TPU v7x, 32 devices: a whole 2x2x4 slice. The times are simulated.
32 devices in a mesh: member: 2 (over x), node: 16 (over z, y, core).
Axes of the slice: x: 2, y: 2, z: 4, core: 2. Of those that a mesh axis runs over, the one named last changes fastest.
Arguments:
- conditioning: bfloat16 [168, 32768], P(None, ('member', 'node')), parts along dimension 1, may hold values from -6 to 6
- target_state: float32 [84, 32768], P(None, ('member', 'node')), parts along dimension 1, may hold values from -6 to 6
- noise_sample: float32 [84, 32768], P(None, ('member', 'node')), parts along dimension 1, may hold values from -6 to 6
- step_index: int32 [2], P('member'), parts along dimension 0, may hold values from 0 to 19
- mesh_features: float32 [3, 10240], P(None, 'node'), may hold values from -1 to 1
- edge_geometry: float32 [4, 65536], P(None, 'node'), may hold values from -6 to 6
- edge_slot: int32 [65536], P('node'), may hold values from 0 to 255, as said below
- edge_receiver: int32 [65536], P('node'), may hold values from 0 to 639
- send_rows: int32 [256, 16], P('node'), may hold values from 0 to 1023
- edge_count: int32 [16], P('node'), may hold values from 1399 to 4096, as said below
- embed_weight: bfloat16 [252, 512], replicated, may hold values from -0.375 to 0.375
- mesh_weight: float32 [3, 512], replicated, may hold values from -3.5 to 3.5
- geom_weight: float32 [4, 512], replicated, may hold values from -3 to 3
- sender_weight: bfloat16 [512, 512], P('node'), may hold values from -0.15625 to 0.15625
- edge_weight: bfloat16 [512, 512], P('node'), may hold values from -0.15625 to 0.15625
- receiver_weight: bfloat16 [512, 512], P('node'), may hold values from -0.15625 to 0.15625
- message_weight: bfloat16 [512, 512], P('node'), may hold values from -0.25 to 0.25
- node_weight: bfloat16 [1024, 512], P('node'), may hold values from -0.1875 to 0.1875
- output_weight: bfloat16 [512, 512], P('node'), may hold values from -0.25 to 0.25
- noise_weight: float32 [32, 512], replicated, may hold values from -1 to 1
- film_weight: bfloat16 [512, 2048], replicated, may hold values from -0.25 to 0.25
Outputs:
- mesh_latent: bfloat16 [10240, 1024], P('node', 'member'), parts along dimension 1
There are 2 independent parts, one for each index of `member`. A program takes and returns all parts, laid end to end along the dimension named above; an argument that names none is the same for every part. Nothing has to cross between parts.
Inputs may be any that keep to these rules, and one draw needn't show every extreme that they name: `edge_slot`: on each device, the live slots name every entry of its 16 * 16 list at least once, or as many distinct entries as there are live slots where these are fewer. `edge_count`: the counts sum to 16 * 2048 and one device has all 4096 slots live.
All inputs are finite; a program needn't handle non-finite values.
Results may differ from a plain program's by a relative error of at most 0.0071.
Values may be sent and summed in bfloat16 or wider, within the bound.
A program may use at most 64 MiB of HBM per device.

v0:
```python
import jax
import jax.numpy as jnp
from jax import lax
from jax.sharding import PartitionSpec as P

STEPS = 20


sigma_top = 80.0
sigma_low = 0.03
rho_power = 7.0
norm_eps = 1e-05


def layer_norm(values):
    mean = jnp.mean(values, axis=-1, keepdims=True)
    centred = values - mean
    var = jnp.mean(centred * centred, axis=-1, keepdims=True)
    return centred * lax.rsqrt(var + norm_eps)


def embed_columns(inputs, embed_weight):
    product = lax.dot_general(
        inputs, embed_weight, (((0,), (0,)), ((), ())), preferred_element_type=jnp.float32
    )
    return jax.nn.silu(product).astype(jnp.bfloat16)


def per_device(
    conditioning,
    target_state,
    noise_sample,
    step_index,
    mesh_features,
    edge_geometry,
    edge_slot,
    edge_receiver,
    send_rows,
    edge_count,
    embed_weight,
    mesh_weight,
    geom_weight,
    sender_weight,
    edge_weight,
    receiver_weight,
    message_weight,
    node_weight,
    output_weight,
    noise_weight,
    film_weight,
):
    width = embed_weight.shape[1]
    freqs = noise_weight.shape[0] // 2
    steps_total = STEPS
    frac = step_index[0].astype(jnp.float32) / (steps_total - 1)
    upper = sigma_top ** (1.0 / rho_power)
    lower = sigma_low ** (1.0 / rho_power)
    sigma = (upper + frac * (lower - upper)) ** rho_power
    angle = 0.25 * jnp.log(sigma) * (jnp.arange(freqs, dtype=jnp.float32) + 1.0)
    fourier = jnp.concatenate([jnp.sin(angle), jnp.cos(angle)])[None, :]
    cond = jax.nn.silu(jnp.dot(fourier, noise_weight, precision=lax.Precision.HIGHEST)).astype(
        jnp.bfloat16
    )
    film = jnp.dot(cond, film_weight, preferred_element_type=jnp.float32)
    edge_scale = film[:, 0:width]
    edge_shift = film[:, width : 2 * width]
    node_scale = film[:, 2 * width : 3 * width]
    node_shift = film[:, 3 * width : 4 * width]
    full_sender, full_edge, full_recv, full_message, full_node, full_output = (
        lax.all_gather(sender_weight, "node", axis=0, tiled=True),
        lax.all_gather(edge_weight, "node", axis=0, tiled=True),
        lax.all_gather(receiver_weight, "node", axis=0, tiled=True),
        lax.all_gather(message_weight, "node", axis=0, tiled=True),
        lax.all_gather(node_weight, "node", axis=0, tiled=True),
        lax.all_gather(output_weight, "node", axis=0, tiled=True),
    )
    noisy = ((target_state + sigma * noise_sample) / jnp.sqrt(sigma * sigma + 1.0)).astype(
        jnp.bfloat16
    )
    raw_local = jnp.concatenate([conditioning, noisy], axis=0)
    picked_rows = send_rows.reshape(-1)
    outgoing_inputs = raw_local[:, picked_rows]
    arrived = lax.all_to_all(outgoing_inputs, "node", split_axis=1, concat_axis=1, tiled=True)
    received = embed_columns(arrived, embed_weight)
    mesh_embed = jax.nn.silu(
        jnp.dot(mesh_features.T, mesh_weight, precision=lax.Precision.HIGHEST)
    ).astype(jnp.bfloat16)
    recv_proj = jnp.dot(mesh_embed, full_recv, preferred_element_type=jnp.float32).astype(
        jnp.bfloat16
    )
    mesh_count = mesh_embed.shape[0]
    slot_count = edge_slot.shape[0]
    block = min(512, slot_count)
    node_ids = jnp.arange(mesh_count, dtype=jnp.int32)
    count = edge_count[0]
    live_blocks = (count + block - 1) // block

    def add_block(index, total):
        start = (index * block).astype(jnp.int32)
        slots = lax.dynamic_slice_in_dim(edge_slot, start, block, 0)
        local_recv = lax.dynamic_slice_in_dim(edge_receiver, start, block, 0)
        geometry = lax.dynamic_slice_in_dim(edge_geometry, start, block, 1)
        embed_rows = jax.nn.silu(
            jnp.dot(geometry.T, geom_weight, precision=lax.Precision.HIGHEST)
        ).astype(jnp.bfloat16)
        one_hot = (local_recv[:, None] == node_ids[None, :]).astype(jnp.bfloat16)
        sender_rows = received[slots]
        pre = jnp.dot(embed_rows, full_edge, preferred_element_type=jnp.float32)
        pre = pre + jnp.dot(sender_rows, full_sender, preferred_element_type=jnp.float32)
        pre = pre + jnp.dot(one_hot, recv_proj, preferred_element_type=jnp.float32)
        hidden = jax.nn.silu(pre).astype(jnp.bfloat16)
        mixed = jnp.dot(hidden, full_message, preferred_element_type=jnp.float32)
        message = layer_norm(mixed) * (1.0 + edge_scale) + edge_shift
        live = start + jnp.arange(block, dtype=jnp.int32) < count
        message = jnp.where(live[:, None], message, 0.0).astype(jnp.bfloat16)
        return total + lax.dot_general(
            one_hot, message, (((0,), (0,)), ((), ())), preferred_element_type=jnp.float32
        )

    zeros_total = jnp.zeros((mesh_count, width), jnp.float32)
    summed = lax.fori_loop(0, live_blocks, add_block, zeros_total)
    gathered = summed.astype(jnp.bfloat16)
    joined = jnp.concatenate([mesh_embed, gathered], axis=1)
    update = jax.nn.silu(jnp.dot(joined, full_node, preferred_element_type=jnp.float32)).astype(
        jnp.bfloat16
    )
    result = jnp.dot(update, full_output, preferred_element_type=jnp.float32)
    return (
        mesh_embed.astype(jnp.float32) + layer_norm(result) * (1.0 + node_scale) + node_shift
    ).astype(jnp.bfloat16)


def solution(mesh):
    placed = (
        P(None, ("member", "node")),
        P(None, ("member", "node")),
        P(None, ("member", "node")),
        P("member"),
        P(None, "node"),
        P(None, "node"),
        P("node"),
        P("node"),
        P("node", None),
        P("node"),
        P(),
        P(),
        P(),
        P("node", None),
        P("node", None),
        P("node", None),
        P("node", None),
        P("node", None),
        P("node", None),
        P(),
        P(),
    )
    return jax.shard_map(
        per_device, mesh=mesh, in_specs=placed, out_specs=P("node", "member"), check_vma=False
    )
```

profile of v0, /device:TPU:19, one launch (start us, length us, event | category | flops | bytes accessed | tf_op | source)
XLA Modules:
  0.0 273.7 jit_solution(12059262301031847272)
XLA Ops:
  7.4 1.1 divide_convert_fusion
  9.3 1.8 gather_fusion.1
  11.1 6.6 %all-to-all-start = ((bf16[252,16,16]{0,2,1:T(8,128)(2,1)}), bf16[252,16,16]{0,2,1:T(8,128)(2,1)S(1)}, u32[]{:S(2)}, u32[]{:S(2)}) async-start(bf16[252,16,16]{0,2,1:T(8,128)(2,1)} %bitcast.4), calls=%async_computation | async-start | bytes 262144 | tf_op jit(solution)/shard_map/all_to_all | solution.py:83
  19.9 18.0 %all_gather.20 = bf16[512,512]{1,0:T(8,128)(2,1)S(1)} all-gather(bf16[32,512]{1,0:T(8,128)(2,1)S(1)} %copy-done.6), channel_id=1, replica_groups=mesh['member'=2,'node'=16] {'node'}, dimensions={0}, use_global_device_ids=true | all-gather | bytes 557056 | tf_op jit(solution)/shard_map/all_gather | solution.py:72
  37.9 20.3 %all_gather.18 = bf16[512,512]{1,0:T(8,128)(2,1)} all-gather(bf16[32,512]{1,0:T(8,128)(2,1)S(1)} %copy-done.7), channel_id=1, replica_groups=mesh['member'=2,'node'=16] {'node'}, dimensions={0}, use_global_device_ids=true | all-gather | bytes 557056 | tf_op jit(solution)/shard_map/all_gather | solution.py:71
  58.2 22.8 %all_gather.19 = bf16[512,512]{1,0:T(8,128)(2,1)} all-gather(bf16[32,512]{1,0:T(8,128)(2,1)S(1)} %copy-done.8), channel_id=1, replica_groups=mesh['member'=2,'node'=16] {'node'}, dimensions={0}, use_global_device_ids=true | all-gather | bytes 557056 | tf_op jit(solution)/shard_map/all_gather | solution.py:70
  81.0 20.6 %all_gather.21 = bf16[512,512]{1,0:T(8,128)(2,1)} all-gather(bf16[32,512]{1,0:T(8,128)(2,1)S(1)} %copy-done.9), channel_id=1, replica_groups=mesh['member'=2,'node'=16] {'node'}, dimensions={0}, use_global_device_ids=true | all-gather | bytes 557056 | tf_op jit(solution)/shard_map/all_gather | solution.py:73
  101.6 1.4 multiply_convert_fusion.3
  103.1 0.8 copy-done.2
  103.9 1.4 convolution_convert_fusion
  105.3 21.3 %all_gather.23 = bf16[512,512]{1,0:T(8,128)(2,1)} all-gather(bf16[32,512]{1,0:T(8,128)(2,1)S(1)} %copy-done.10), channel_id=1, replica_groups=mesh['member'=2,'node'=16] {'node'}, dimensions={0}, use_global_device_ids=true | all-gather | bytes 557056 | tf_op jit(solution)/shard_map/all_gather | solution.py:75
  126.9 1.2 broadcast_in_dim.12
  128.2 127.9 %while.11 = (s32[]{:T(128)}, f32[640,512]{1,0:T(8,128)}, s32[]{:T(128)}, s32[4096]{0:T(1024)}, s32[]{:T(128)}, /*index=5*/f32[4,4096]{1,0:T(4,128)}, f32[4,512]{...) while((s32[]{:T(128)}, f32[640,512]{1,0:T(8,128)}, ...), condition=%wide.region_3.4_spmd.clone, body=%wide.region_0.3_spmd.clone.sunk | while | flops 1496060416 | bytes 16973068 | solution.py:121
  128.2 1.9 multiply_convert_fusion.6
  130.5 0.8 compare_select_fusion.3
  131.3 2.6 gather_fusion
  134.0 2.6 convolution_add_fusion.5
  137.3 2.7 %fusion.84 = (f32[512]{0:T(512)S(1)}, f32[512,512]{0,1:T(8,128)S(1)}) fusion(bf16[512,512]{1,0:T(8,128)(2,1)} %get-tuple-element.308, f32[512,512]{1,0:T(8,128)} %convolution_add_fusion.5, bf16[640,512]{1,0:T(8,128)(2,1)} %get-tuple-element.307, s32[512]{0:T(512)S(1)} %dynamic_slice.20), kind=kOutput, calls=%fused_computation.63.clone.1 | convolution fusion | flops 606141952 | bytes 3280896 | tf_op jit(solution)/shard_map/while/body/dot_general | solution.py:112
  141.0 3.2 %convolution_add_fusion.6 = f32[640,512]{1,0:T(8,128)} fusion(f32[640,512]{1,0:T(8,128)} %get-tuple-element.278, s32[512]{0:T(512)S(1)} %dynamic_slice.20, f32[512,512]{0,1:T(8,128)S(1)} %get-tuple-element.256, f32[512]{0:T(512)S(1)} %bitcast.56, f32[512]{0:T(512)S(1)} %bitcast.54, f32[512]{0:T(512)S(1)} %add_rsqrt_fusion.3, ...), kind=kOutput, calls=%fused_computation.3.clone.1 | convolution fusion | flops 338100224 | bytes 3680768 | tf_op jit(solution)/shard_map/while/body/dot_general | solution.py:116
  144.2 1.9 multiply_convert_fusion.6
  146.5 0.8 compare_select_fusion.3
  147.3 2.6 gather_fusion
  149.9 2.6 convolution_add_fusion.5
  153.3 2.7 %fusion.84 = (f32[512]{0:T(512)S(1)}, f32[512,512]{0,1:T(8,128)S(1)}) fusion(bf16[512,512]{1,0:T(8,128)(2,1)} %get-tuple-element.308, f32[512,512]{1,0:T(8,128)} %convolution_add_fusion.5, bf16[640,512]{1,0:T(8,128)(2,1)} %get-tuple-element.307, s32[512]{0:T(512)S(1)} %dynamic_slice.20), kind=kOutput, calls=%fused_computation.63.clone.1 | convolution fusion | flops 606141952 | bytes 3280896 | tf_op jit(solution)/shard_map/while/body/dot_general | solution.py:112
  156.9 3.2 %convolution_add_fusion.6 = f32[640,512]{1,0:T(8,128)} fusion(f32[640,512]{1,0:T(8,128)} %get-tuple-element.278, s32[512]{0:T(512)S(1)} %dynamic_slice.20, f32[512,512]{0,1:T(8,128)S(1)} %get-tuple-element.256, f32[512]{0:T(512)S(1)} %bitcast.56, f32[512]{0:T(512)S(1)} %bitcast.54, f32[512]{0:T(512)S(1)} %add_rsqrt_fusion.3, ...), kind=kOutput, calls=%fused_computation.3.clone.1 | convolution fusion | flops 338100224 | bytes 3680768 | tf_op jit(solution)/shard_map/while/body/dot_general | solution.py:116
  160.1 1.9 multiply_convert_fusion.6
  162.5 0.8 compare_select_fusion.3
  163.3 2.6 gather_fusion
  165.9 2.6 convolution_add_fusion.5
  169.3 2.7 %fusion.84 = (f32[512]{0:T(512)S(1)}, f32[512,512]{0,1:T(8,128)S(1)}) fusion(bf16[512,512]{1,0:T(8,128)(2,1)} %get-tuple-element.308, f32[512,512]{1,0:T(8,128)} %convolution_add_fusion.5, bf16[640,512]{1,0:T(8,128)(2,1)} %get-tuple-element.307, s32[512]{0:T(512)S(1)} %dynamic_slice.20), kind=kOutput, calls=%fused_computation.63.clone.1 | convolution fusion | flops 606141952 | bytes 3280896 | tf_op jit(solution)/shard_map/while/body/dot_general | solution.py:112
  172.9 3.2 %convolution_add_fusion.6 = f32[640,512]{1,0:T(8,128)} fusion(f32[640,512]{1,0:T(8,128)} %get-tuple-element.278, s32[512]{0:T(512)S(1)} %dynamic_slice.20, f32[512,512]{0,1:T(8,128)S(1)} %get-tuple-element.256, f32[512]{0:T(512)S(1)} %bitcast.56, f32[512]{0:T(512)S(1)} %bitcast.54, f32[512]{0:T(512)S(1)} %add_rsqrt_fusion.3, ...), kind=kOutput, calls=%fused_computation.3.clone.1 | convolution fusion | flops 338100224 | bytes 3680768 | tf_op jit(solution)/shard_map/while/body/dot_general | solution.py:116
  176.1 1.9 multiply_convert_fusion.6
  178.5 0.8 compare_select_fusion.3
  179.3 2.6 gather_fusion
  181.9 2.6 convolution_add_fusion.5
  185.3 2.7 %fusion.84 = (f32[512]{0:T(512)S(1)}, f32[512,512]{0,1:T(8,128)S(1)}) fusion(bf16[512,512]{1,0:T(8,128)(2,1)} %get-tuple-element.308, f32[512,512]{1,0:T(8,128)} %convolution_add_fusion.5, bf16[640,512]{1,0:T(8,128)(2,1)} %get-tuple-element.307, s32[512]{0:T(512)S(1)} %dynamic_slice.20), kind=kOutput, calls=%fused_computation.63.clone.1 | convolution fusion | flops 606141952 | bytes 3280896 | tf_op jit(solution)/shard_map/while/body/dot_general | solution.py:112
  188.9 3.2 %convolution_add_fusion.6 = f32[640,512]{1,0:T(8,128)} fusion(f32[640,512]{1,0:T(8,128)} %get-tuple-element.278, s32[512]{0:T(512)S(1)} %dynamic_slice.20, f32[512,512]{0,1:T(8,128)S(1)} %get-tuple-element.256, f32[512]{0:T(512)S(1)} %bitcast.56, f32[512]{0:T(512)S(1)} %bitcast.54, f32[512]{0:T(512)S(1)} %add_rsqrt_fusion.3, ...), kind=kOutput, calls=%fused_computation.3.clone.1 | convolution fusion | flops 338100224 | bytes 3680768 | tf_op jit(solution)/shard_map/while/body/dot_general | solution.py:116
  192.1 1.9 multiply_convert_fusion.6
  194.5 0.8 compare_select_fusion.3
  195.3 2.6 gather_fusion
  197.9 2.6 convolution_add_fusion.5
  201.3 2.7 %fusion.84 = (f32[512]{0:T(512)S(1)}, f32[512,512]{0,1:T(8,128)S(1)}) fusion(bf16[512,512]{1,0:T(8,128)(2,1)} %get-tuple-element.308, f32[512,512]{1,0:T(8,128)} %convolution_add_fusion.5, bf16[640,512]{1,0:T(8,128)(2,1)} %get-tuple-element.307, s32[512]{0:T(512)S(1)} %dynamic_slice.20), kind=kOutput, calls=%fused_computation.63.clone.1 | convolution fusion | flops 606141952 | bytes 3280896 | tf_op jit(solution)/shard_map/while/body/dot_general | solution.py:112
  204.9 3.2 %convolution_add_fusion.6 = f32[640,512]{1,0:T(8,128)} fusion(f32[640,512]{1,0:T(8,128)} %get-tuple-element.278, s32[512]{0:T(512)S(1)} %dynamic_slice.20, f32[512,512]{0,1:T(8,128)S(1)} %get-tuple-element.256, f32[512]{0:T(512)S(1)} %bitcast.56, f32[512]{0:T(512)S(1)} %bitcast.54, f32[512]{0:T(512)S(1)} %add_rsqrt_fusion.3, ...), kind=kOutput, calls=%fused_computation.3.clone.1 | convolution fusion | flops 338100224 | bytes 3680768 | tf_op jit(solution)/shard_map/while/body/dot_general | solution.py:116
  208.1 1.9 multiply_convert_fusion.6
  210.5 0.8 compare_select_fusion.3
  211.3 2.6 gather_fusion
  213.9 2.6 convolution_add_fusion.5
  217.3 2.7 %fusion.84 = (f32[512]{0:T(512)S(1)}, f32[512,512]{0,1:T(8,128)S(1)}) fusion(bf16[512,512]{1,0:T(8,128)(2,1)} %get-tuple-element.308, f32[512,512]{1,0:T(8,128)} %convolution_add_fusion.5, bf16[640,512]{1,0:T(8,128)(2,1)} %get-tuple-element.307, s32[512]{0:T(512)S(1)} %dynamic_slice.20), kind=kOutput, calls=%fused_computation.63.clone.1 | convolution fusion | flops 606141952 | bytes 3280896 | tf_op jit(solution)/shard_map/while/body/dot_general | solution.py:112
  220.9 3.2 %convolution_add_fusion.6 = f32[640,512]{1,0:T(8,128)} fusion(f32[640,512]{1,0:T(8,128)} %get-tuple-element.278, s32[512]{0:T(512)S(1)} %dynamic_slice.20, f32[512,512]{0,1:T(8,128)S(1)} %get-tuple-element.256, f32[512]{0:T(512)S(1)} %bitcast.56, f32[512]{0:T(512)S(1)} %bitcast.54, f32[512]{0:T(512)S(1)} %add_rsqrt_fusion.3, ...), kind=kOutput, calls=%fused_computation.3.clone.1 | convolution fusion | flops 338100224 | bytes 3680768 | tf_op jit(solution)/shard_map/while/body/dot_general | solution.py:116
  224.1 1.9 multiply_convert_fusion.6
  227.2 2.6 gather_fusion
  229.9 2.6 convolution_add_fusion.5
  233.3 2.7 %fusion.84 = (f32[512]{0:T(512)S(1)}, f32[512,512]{0,1:T(8,128)S(1)}) fusion(bf16[512,512]{1,0:T(8,128)(2,1)} %get-tuple-element.308, f32[512,512]{1,0:T(8,128)} %convolution_add_fusion.5, bf16[640,512]{1,0:T(8,128)(2,1)} %get-tuple-element.307, s32[512]{0:T(512)S(1)} %dynamic_slice.20), kind=kOutput, calls=%fused_computation.63.clone.1 | convolution fusion | flops 606141952 | bytes 3280896 | tf_op jit(solution)/shard_map/while/body/dot_general | solution.py:112
  236.9 3.2 %convolution_add_fusion.6 = f32[640,512]{1,0:T(8,128)} fusion(f32[640,512]{1,0:T(8,128)} %get-tuple-element.278, s32[512]{0:T(512)S(1)} %dynamic_slice.20, f32[512,512]{0,1:T(8,128)S(1)} %get-tuple-element.256, f32[512]{0:T(512)S(1)} %bitcast.56, f32[512]{0:T(512)S(1)} %bitcast.54, f32[512]{0:T(512)S(1)} %add_rsqrt_fusion.3, ...), kind=kOutput, calls=%fused_computation.3.clone.1 | convolution fusion | flops 338100224 | bytes 3680768 | tf_op jit(solution)/shard_map/while/body/dot_general | solution.py:116
  240.1 1.9 multiply_convert_fusion.6
  243.2 2.6 gather_fusion
  245.9 2.6 convolution_add_fusion.5
  249.2 2.7 %fusion.84 = (f32[512]{0:T(512)S(1)}, f32[512,512]{0,1:T(8,128)S(1)}) fusion(bf16[512,512]{1,0:T(8,128)(2,1)} %get-tuple-element.308, f32[512,512]{1,0:T(8,128)} %convolution_add_fusion.5, bf16[640,512]{1,0:T(8,128)(2,1)} %get-tuple-element.307, s32[512]{0:T(512)S(1)} %dynamic_slice.20), kind=kOutput, calls=%fused_computation.63.clone.1 | convolution fusion | flops 606141952 | bytes 3280896 | tf_op jit(solution)/shard_map/while/body/dot_general | solution.py:112
  252.9 3.2 %convolution_add_fusion.6 = f32[640,512]{1,0:T(8,128)} fusion(f32[640,512]{1,0:T(8,128)} %get-tuple-element.278, s32[512]{0:T(512)S(1)} %dynamic_slice.20, f32[512,512]{0,1:T(8,128)S(1)} %get-tuple-element.256, f32[512]{0:T(512)S(1)} %bitcast.56, f32[512]{0:T(512)S(1)} %bitcast.54, f32[512]{0:T(512)S(1)} %add_rsqrt_fusion.3, ...), kind=kOutput, calls=%fused_computation.3.clone.1 | convolution fusion | flops 338100224 | bytes 3680768 | tf_op jit(solution)/shard_map/while/body/dot_general | solution.py:116
  256.1 2.4 copy.31
  258.5 3.9 %fusion.40 = (f32[640]{0:T(1024)S(1)}, f32[640,512]{0,1:T(8,128)S(1)}) fusion(bf16[512,512]{1,0:T(8,128)(2,1)} %all_gather.23, bf16[1024,512]{1,0:T(8,128)(2,1)} %all-gather.2.cloned.1.call-done, bf16[640,512]{0,1:T(8,128)(2,1)} %copy.31, bf16[640,512]{0,1:T(8,128)(2,1)} %copy-done.2), kind=kOutput, calls=%fused_computation.64 | convolution fusion | flops 1011219840 | bytes 4196864 | tf_op jit(solution)/shard_map/dot_general | solution.py:127
  262.6 0.9 copy-done.3
  263.5 1.2 add_convert_fusion
  264.6 2.2 copy.34
  (130 shorter events, 20.6 us)
Async XLA Ops:
  6.5 12.9 %copy-start = (bf16[512,2048]{1,0:T(8,128)(2,1)S(1)}, bf16[512,2048]{1,0:T(8,128)(2,1)}, u32[]{:S(2)}) copy-start(bf16[512,2048]{1,0:T(8,128)(2,1)} %param.43) | copy-start | bytes 6291460
  6.5 2.2 copy-start.4
  6.5 2.4 copy-start.11
  9.1 10.1 %copy-start.5 = (f32[32,512]{1,0:T(8,128)S(1)}, f32[32,512]{1,0:T(8,128)}, u32[]{:S(2)}) copy-start(f32[32,512]{1,0:T(8,128)} %param.42) | copy-start | bytes 196612
  11.1 8.8 %copy-start.6 = (bf16[32,512]{1,0:T(8,128)(2,1)S(1)}, bf16[32,512]{1,0:T(8,128)(2,1)}, u32[]{:S(2)}) copy-start(bf16[32,512]{1,0:T(8,128)(2,1)} %param.38) | copy-start | bytes 98308
  11.1 115.5 %all-to-all-start = ((bf16[252,16,16]{0,2,1:T(8,128)(2,1)}), bf16[252,16,16]{0,2,1:T(8,128)(2,1)S(1)}, u32[]{:S(2)}, u32[]{:S(2)}) async-start(bf16[252,16,16]{0,2,1:T(8,128)(2,1)} %bitcast.4), calls=%async_computation | async-start | bytes 262144 | tf_op jit(solution)/shard_map/all_to_all | solution.py:83
  17.7 240.8 %all-gather.2.cloned.1.call-start = ((), (), s32[]{:S(2)}) async-start(), calls=%async_computation.1 | async-start | bytes 1114112 | tf_op jit(solution)/shard_map/all_gather | solution.py:74
  19.4 18.4 %copy-start.7 = (bf16[32,512]{1,0:T(8,128)(2,1)S(1)}, bf16[32,512]{1,0:T(8,128)(2,1)}, u32[]{:S(2)}) copy-start(bf16[32,512]{1,0:T(8,128)(2,1)} %param.37) | copy-start | bytes 98308
  19.4 38.8 %copy-start.8 = (bf16[32,512]{1,0:T(8,128)(2,1)S(1)}, bf16[32,512]{1,0:T(8,128)(2,1)}, u32[]{:S(2)}) copy-start(bf16[32,512]{1,0:T(8,128)(2,1)} %param.36) | copy-start | bytes 98308
  19.8 61.2 %copy-start.9 = (bf16[32,512]{1,0:T(8,128)(2,1)S(1)}, bf16[32,512]{1,0:T(8,128)(2,1)}, u32[]{:S(2)}) copy-start(bf16[32,512]{1,0:T(8,128)(2,1)} %param.39) | copy-start | bytes 98308
  19.8 81.8 %copy-start.13 = (f32[3,640]{1,0:T(4,128)S(1)}, f32[3,640]{1,0:T(4,128)}, u32[]{:S(2)}) copy-start(f32[3,640]{1,0:T(4,128)} %param.27) | copy-start | bytes 23044
  19.8 81.8 %copy-start.14 = (f32[3,512]{1,0:T(4,128)S(1)}, f32[3,512]{1,0:T(4,128)}, u32[]{:S(2)}) copy-start(f32[3,512]{1,0:T(4,128)} %param.34) | copy-start | bytes 18436
  103.0 0.8 copy-start.2
  103.9 1.4 copy-start.10
  103.9 22.7 %copy-start.12 = (bf16[252,512]{1,0:T(8,128)(2,1)S(1)}, bf16[252,512]{1,0:T(8,128)(2,1)}, u32[]{:S(2)}) copy-start(bf16[252,512]{1,0:T(8,128)(2,1)} %param.33) | copy-start | bytes 774148
  126.9 1.3 copy-start.15
  128.2 1.9 copy-start.1
  144.1 1.9 copy-start.1
  160.1 1.9 copy-start.1
  176.1 1.9 copy-start.1
  192.1 1.9 copy-start.1
  208.1 1.9 copy-start.1
  224.1 1.9 copy-start.1
  240.1 1.9 copy-start.1
  262.4 1.1 copy-start.3
Sparse Core Ops, SparseCore 0:
  20.6 37.7 all-gather.1
where the time goes:
time: 276 us; the launch traced here: 274 us
  blocking collectives  103 us (37%)
  matrix products  94.8 us (34%)
  local copies, waits for them, and re-layouts  37.1 us (13%)
  other arithmetic  15.8 us (6%)
  between operations  15.2 us (6%)
  starting transfers between devices  6.63 us (2%)
    dot_general x8, matrix products, add_block(): lax.dot_general(one_hot, message, (((0,), (0,)), ((), ())), preferred_ele...  25.5 us
    all_gather x1, blocking collectives, per_device(): lax.all_gather(sender_weight, 'node', axis=0, tiled=True)  22.8 us
    dot_general x8, matrix products, add_block(): mixed = jnp.dot(hidden, full_message, preferred_element_type=jnp.float32)  22 us
    all_gather x1, blocking collectives, per_device(): lax.all_gather(output_weight, 'node', axis=0, tiled=True)  21.3 us
    gather x8, local copies, waits for them, and re-layouts, add_block(): sender_rows = received[slots]  21.1 us
    dot_general x8, matrix products, add_block(): jnp.dot(sender_rows, full_sender, preferred_element_type=jnp.float32)  20.9 us
    all_gather x1, blocking collectives, per_device(): lax.all_gather(message_weight, 'node', axis=0, tiled=True)  20.6 us
    all_gather x1, blocking collectives, per_device(): lax.all_gather(edge_weight, 'node', axis=0, tiled=True)  20.3 us
  transfers between devices with their start and end apart: 2, of which 0 were waited for; matrix products, arithmetic and copies ran while one was open for 49% of the time, Pallas kernels for 0%

commit v1 on v0

v1 whole, which is shorter than its diff:
```python
import functools

import jax
import jax.numpy as jnp
from jax import lax
from jax.experimental import pallas as pl
from jax.experimental.pallas import tpu as pltpu
from jax.sharding import PartitionSpec as P

STEPS = 20


sigma_top = 80.0
sigma_low = 0.03
rho_power = 7.0
norm_eps = 1e-05
f32, bf16 = jnp.float32, jnp.bfloat16


def is_folded(mesh):
    rows = mesh.devices[0]
    places = [getattr(device, "coords", None) for device in rows[:5:2]]
    if len(places) < 3 or any(place is None for place in places):
        return False
    first = [a != b for a, b in zip(places[0], places[1])]
    second = [a != b for a, b in zip(places[0], places[2])]
    return first != second


def silu(x):
    half = 0.5 * x
    return half * jnp.tanh(half) + half


def outer_sum(columns, rows):
    total = columns[:, 0:1] * rows[0:1, :]
    for index in range(1, rows.shape[0]):
        total = total + columns[:, index : index + 1] * rows[index : index + 1, :]
    return total


def normalised(values):
    mean = jnp.mean(values, axis=0, keepdims=True)
    centred = values - mean
    var = jnp.mean(centred * centred, axis=0, keepdims=True)
    return centred * lax.rsqrt(var + norm_eps)


def nn(a, b):
    return jnp.dot(a, b, preferred_element_type=f32)


def nt(a, b):
    return lax.dot_general(a, b, (((1,), (1,)), ((), ())), preferred_element_type=f32)


def encoder_kernel(n, folded, block, *refs):
    step_ref, count_ref, slot_ref, recv_ref, rows_ref, geom_ref, mesh_ref = refs[:7]
    cond_ref, target_ref, noise_ref, embed_ref, mesh_w_ref, geom_w_ref, noise_w_ref, film_w_ref = refs[7:15]
    shards, out_ref = refs[15:21], refs[21]
    fulls = refs[22:28]
    picked_ref, outgoing, arrived, embed_pad_ref, cols_ref, edges_ref = refs[28:34]
    table_ref, edge_t_ref, message_t_ref, embed_t_ref, total_ref = refs[34:39]
    send_sem, recv_sem, psend_sem, precv_sem, asend_sem, arecv_sem, own_sem = refs[39:]
    me = lax.axis_index("node")
    core, chip = me % 2, me // 2
    partner = chip * 2 + 1 - core
    chips = n // 2
    half = chips // 2

    def same(index):
        return index

    if folded:

        def to_pos(c):
            z, y = c // 2, c % 2
            return z + y * (chips - 1 - 2 * z)

        def to_chip(p):
            y = p // half
            return (p + y * (chips - 1 - 2 * p)) * 2 + y
    else:
        to_pos = to_chip = same

    pos = to_pos(chip)

    def device_at(shift):
        return to_chip((pos + shift + chips) % chips) * 2 + core

    sent = []

    def remote(source, target, send, recv, device):
        copy = pltpu.make_async_remote_copy(
            src_ref=source, dst_ref=target, send_sem=send, recv_sem=recv, device_id={"node": device}
        )
        copy.start()
        sent.append(copy)
        return copy

    long, short = chips // 2, chips - 1 - chips // 2
    reach = [[long, short] if k % 2 == 0 else [short, long] for k in range(6)]
    ring = {}
    passed = {k: [] for k in range(6)}
    early, late = (0, 1, 2, 3), (4, 5)

    def relay(group, step):
        onward = []
        for k in group:
            for side in (0, 1):
                way = 1 - 2 * side
                last = reach[k][side]
                if step > last + 1:
                    continue
                block_at = device_at(-way * (step - 1))
                target = fulls[k].at[block_at]
                source = shards[k] if step == 1 else target
                if step > 1:
                    ring[k, side, step - 1].wait_recv()
                if step <= last:
                    ring[k, side, step] = remote(
                        source,
                        target,
                        send_sem.at[k, side, step],
                        recv_sem.at[k, side, step],
                        device_at(way),
                    )
                if step > 1 or side == 0:
                    index = side * (long + 1) + step - 1
                    onward.append((k, index, source, target))
        for k, index, source, target in onward:
            passed[k].append(
                remote(source, target, psend_sem.at[k, index], precv_sem.at[k, index], partner)
            )

    barrier = pltpu.get_barrier_semaphore()
    for step in range(1, n):
        pl.semaphore_signal(barrier, inc=1, device_id={"node": (me + step) % n})
    own = []
    for k in range(6):
        own.append(pltpu.make_async_copy(shards[k], fulls[k].at[me], own_sem.at[k]))
        own[k].start()
    pl.semaphore_wait(barrier, n - 1)
    relay(early, 1)

    width = embed_ref.shape[1]
    channels = embed_ref.shape[0]
    cap = outgoing.shape[1]
    frac = jnp.full((1, 1), step_ref[0], jnp.int32).astype(f32) / (STEPS - 1)
    upper = sigma_top ** (1.0 / rho_power)
    lower = sigma_low ** (1.0 / rho_power)
    root = upper + frac * (lower - upper)
    cube = root * root * root
    sigma = cube * cube * root
    noisy = ((target_ref[...] + sigma * noise_ref[...]) / jnp.sqrt(sigma * sigma + 1.0)).astype(bf16)
    points, listed = cond_ref.shape[1], rows_ref.shape[1]
    fixed = cond_ref.shape[0]
    pick = lax.broadcasted_iota(jnp.int32, (points, listed), 0) == rows_ref[...]
    pick = pick.astype(f32).astype(bf16)
    picked_ref[...] = jnp.zeros_like(picked_ref)
    picked_ref[:fixed, :] = nn(cond_ref[...], pick)
    picked_ref[fixed:channels, :] = nn(noisy, pick)
    outgoing[...] = picked_ref[...].T.astype(bf16).reshape(outgoing.shape)
    relay(early, 2)

    freqs = noise_w_ref.shape[0] // 2
    place_k = lax.broadcasted_iota(jnp.int32, (2 * freqs, 1), 0)
    wave = (place_k % freqs + 1).astype(f32)
    angle = 0.25 * jnp.log(sigma) * wave
    fourier = jnp.where(place_k < freqs, jnp.sin(angle), jnp.cos(angle))
    cond = silu(jnp.sum(fourier * noise_w_ref[...], axis=0, keepdims=True)).astype(bf16)
    film = nn(cond, film_w_ref[...])
    small = [film[:, width * i : width * (i + 1)] for i in range(4)]
    geoms, feats = geom_w_ref.shape[0], mesh_w_ref.shape[0]
    small += [geom_w_ref[i : i + 1, :] for i in range(geoms)]
    small += [mesh_w_ref[i : i + 1, :] for i in range(feats)]
    line = lax.broadcasted_iota(jnp.int32, (128, width), 0)
    stacked = jnp.zeros((128, width), f32)
    for i, row in enumerate(small):
        stacked = jnp.where(line == i, row, stacked)
    cols_ref[...] = stacked.T
    geom_cols = cols_ref[:, 4 : 4 + geoms]
    mesh_cols = cols_ref[:, 4 + geoms : 4 + geoms + feats]
    mesh_embed = silu(outer_sum(mesh_cols, mesh_ref[...])).astype(bf16)
    embed_t_ref[...] = mesh_embed

    own.append(pltpu.make_async_copy(outgoing.at[me], arrived.at[me], own_sem.at[6]))
    own[6].start()
    swaps = []
    for step in range(1, n):
        other = (me + step) % n
        swaps.append(
            remote(outgoing.at[other], arrived.at[me], asend_sem.at[step], arecv_sem.at[step], other)
        )
    relay(early, 3)
    relay(late, 1)

    blocks = geom_ref.shape[1] // block

    def embed_edges(index, carry):
        here = pl.ds(pl.multiple_of(index * block, block), block)
        edges_ref[index] = silu(outer_sum(geom_cols, geom_ref[:, here])).astype(bf16)
        return carry

    lax.fori_loop(0, blocks // 2, embed_edges, 0)
    relay(early, 4)
    lax.fori_loop(blocks // 2, blocks, embed_edges, 0)
    for step in range(5, long + 2):
        relay(early, step)
    embed_pad_ref[...] = jnp.zeros_like(embed_pad_ref)
    embed_pad_ref[:channels, :] = embed_ref[...]
    for copy in own:
        copy.wait()
    for copy in swaps:
        copy.wait_recv()
    sources = arrived[...].reshape(listed, arrived.shape[2])
    received = silu(nt(embed_pad_ref[...].T, sources)).astype(bf16)

    def full(k):
        return fulls[k][...].reshape(-1, width)

    for k in early:
        for copy in passed[k]:
            copy.wait_recv()
    table_ref[:, :listed] = nn(full(0).T, received).astype(bf16)
    edge_t_ref[...] = full(1).T
    table_ref[:, listed:] = nn(full(2).T, embed_t_ref[...]).astype(bf16)
    message_t_ref[...] = full(3).T
    total_ref[...] = jnp.zeros_like(total_ref)
    nodes = mesh_ref.shape[1]
    count = count_ref[0]

    def add_block(index, carry):
        start = pl.multiple_of(index * block, block)
        here = pl.ds(start, block)
        recv = recv_ref[:, here]
        live = start + lax.broadcasted_iota(jnp.int32, (1, block), 1) < count
        recv = jnp.where(live, recv, -1)
        pick = lax.broadcasted_iota(jnp.int32, (listed, block), 0) == slot_ref[:, here]
        pick = pick.astype(f32).astype(bf16)
        place = lax.broadcasted_iota(jnp.int32, (nodes, block), 0) == recv
        place = place.astype(f32).astype(bf16)
        pre = nn(edge_t_ref[...], edges_ref[index])
        pre = pre + nn(table_ref[:, :listed], pick)
        pre = pre + nn(table_ref[:, listed:], place)
        hidden = silu(pre).astype(bf16)
        mixed = nn(message_t_ref[...], hidden)
        message = normalised(mixed) * (1.0 + cols_ref[:, 0:1]) + cols_ref[:, 1:2]
        total_ref[...] += nt(message.astype(bf16), place)
        return carry

    stages = min(long, blocks)
    for stage in range(stages):
        lax.fori_loop(blocks * stage // stages, blocks * (stage + 1) // stages, add_block, 0)
        relay(late, stage + 2)
    for step in range(stages + 2, long + 2):
        relay(late, step)
    for k in late:
        for copy in passed[k]:
            copy.wait_recv()
    node_t = full(4).T
    update = nn(node_t[:, :width], embed_t_ref[...])
    update = update + nn(node_t[:, width:], total_ref[...].astype(bf16))
    update = silu(update).astype(bf16)
    result = nn(full(5).T, update)
    result = normalised(result) * (1.0 + cols_ref[:, 2:3]) + cols_ref[:, 3:4]
    out_ref[...] = (embed_t_ref[...].astype(f32) + result).T.astype(bf16)
    for copy in sent:
        copy.wait_send()


def per_device(n, folded, *args):
    conditioning, target_state, noise_sample, step_index, mesh_features, edge_geometry = args[:6]
    edge_slot, edge_receiver, send_rows, edge_count, embed_weight, mesh_weight, geom_weight = args[6:13]
    shards, noise_weight, film_weight = args[13:19], args[19], args[20]
    channels, width = embed_weight.shape
    nodes, edges = mesh_features.shape[1], edge_geometry.shape[1]
    cap = send_rows.shape[1]
    listed = n * cap
    deep = channels + -channels % 128
    block = min(512, edges)
    long = n // 4 + 1
    dma = pltpu.SemaphoreType.DMA
    vmem = pl.BlockSpec(memory_space=pltpu.VMEM)
    smem = pl.BlockSpec(memory_space=pltpu.SMEM)
    return pl.pallas_call(
        functools.partial(encoder_kernel, n, folded, block),
        out_shape=jax.ShapeDtypeStruct((nodes, width), bf16),
        in_specs=[smem] * 2 + [vmem] * 19,
        out_specs=vmem,
        scratch_shapes=[pltpu.VMEM((n,) + shard.shape, bf16) for shard in shards]
        + [
            pltpu.VMEM((deep, listed), f32),
            pltpu.VMEM((n, cap, deep), bf16),
            pltpu.VMEM((n, cap, deep), bf16),
            pltpu.VMEM((deep, width), bf16),
            pltpu.VMEM((width, 128), f32),
            pltpu.VMEM((edges // block, width, block), bf16),
            pltpu.VMEM((width, listed + nodes), bf16),
            pltpu.VMEM((width, width), bf16),
            pltpu.VMEM((width, width), bf16),
            pltpu.VMEM((width, nodes), bf16),
            pltpu.VMEM((width, nodes), f32),
            dma((6, 2, long + 1)),
            dma((6, 2, long + 1)),
            dma((6, 2 * (long + 1))),
            dma((6, 2 * (long + 1))),
            dma((n,)),
            dma((n,)),
            dma((7,)),
        ],
        compiler_params=pltpu.CompilerParams(collective_id=0, has_side_effects=True),
    )(
        step_index,
        edge_count,
        edge_slot.reshape(1, -1),
        edge_receiver.reshape(1, -1),
        send_rows.reshape(1, -1),
        edge_geometry,
        mesh_features,
        conditioning,
        target_state,
        noise_sample,
        embed_weight,
        mesh_weight,
        geom_weight,
        noise_weight,
        film_weight,
        *shards,
    )


def solution(mesh):
    placed = (
        P(None, ("member", "node")),
        P(None, ("member", "node")),
        P(None, ("member", "node")),
        P("member"),
        P(None, "node"),
        P(None, "node"),
        P("node"),
        P("node"),
        P("node", None),
        P("node"),
        P(),
        P(),
        P(),
        P("node", None),
        P("node", None),
        P("node", None),
        P("node", None),
        P("node", None),
        P("node", None),
        P(),
        P(),
    )
    n = mesh.shape["node"]
    body = functools.partial(per_device, n, is_folded(mesh))
    return jax.shard_map(
        body, mesh=mesh, in_specs=placed, out_specs=P("node", "member"), check_vma=False
    )
```

time: 276 us -> 56.3 us (0.20)
  the two profiles are of different devices: /device:TPU:19 before, /device:TPU:0 now
where the time goes in v1:
time: 56.3 us; the launch traced here: 56.1 us
  Pallas kernels  51.4 us (91%)
  local copies, waits for them, and re-layouts  3.31 us (6%)
  between operations  1.31 us (2%)
    pallas_call x1, Pallas kernels, per_device(): pl.pallas_call(functools.partial(encoder_kernel, n, folded, block), out_s...  51.4 us
    unnamed x1, local copies, waits for them, and re-layouts  1.97 us
    reshape x1, local copies, waits for them, and re-layouts, per_device(): send_rows.reshape(1, -1)  1.34 us

profile of v1, /device:TPU:0, one launch (start us, length us, event | category | flops | bytes accessed | tf_op | source)
XLA Modules:
  0.0 56.1 jit_solution(7495195195263041622)
XLA Ops:
  1.3 1.3 %reshape.11.refs_4_ = s32[1,256]{1,0:T(1,128)} reshape(s32[16,16]{1,0:T(8,128)} %param.29) | data formatting | bytes 2048 | tf_op jit(solution)/shard_map/reshape | solution.py:318
  2.6 51.4 %shard_map.199 = bf16[640,512]{1,0:T(8,128)(2,1)} custom-call(s32[1]{0:T(128)S(6)} %copy.23.refs_0_, s32[1]{0:T(128)S(6)} %copy.24.refs_1_, s32[1,4096]{1,0:T(1,128)} %bitcast.2, s32[1,4096]{1,0:T(1,128)} %bitcast.3, s32[1,256]{1,0:T(1,128)} %reshape.11.refs_4_, f32[4,4096]{1,0:T(4,128)} %refs_5_.1, f32[3,640]{1,0:T(4,128)} %refs_6_.1, ...), custom_call_target="tpu_custom_call" | custom-call | tf_op jit(solution)/shard_map/pallas_call | solution.py:286
  54.1 2.0 %copy.25 = bf16[640,512]{1,0:T(8,128)(2,1)} copy(bf16[640,512]{1,0:T(8,128)(2,1)} %shard_map.199) | data formatting | bytes 1310720
